TPU v7x, 32 devices: a whole 2x2x4 slice. The times are simulated.
32 devices in a mesh: ep: 8 (over z, x), tp: 4 (over y, core).
Axes of the slice: x: 2, y: 2, z: 4, core: 2. Of those that a mesh axis runs over, the one named last changes fastest.
Arguments:
- tokens: bfloat16 [2048, 2048], P('ep', 'tp'), may hold values from -180 to 180
- norm_gain: float32 [2048], replicated, may hold values from 0.1 to 1.9
- router_weight: bfloat16 [2048, 60], P('tp'), may hold values from -2 to 2
- shared_gate_w: bfloat16 [2048], replicated, may hold values from -0.125 to 0.125
- expert_ids: int32 [2048, 4], P('ep'), may hold values from 0 to 59, all different within a row; in each aligned block of 256 rows (0 to 255, 256 to 511, ...) at most 32 rows name the same one
- w_gate: bfloat16 [64, 2048, 1408], P('ep', None, 'tp'), may hold values from -0.125 to 0.125
- w_up: bfloat16 [64, 2048, 1408], P('ep', None, 'tp'), may hold values from -0.125 to 0.125
- w_down: bfloat16 [64, 1408, 2048], P('ep', 'tp'), may hold values from -1.5 to 1.5
- shared_w_gate: bfloat16 [2048, 2816], P(None, 'tp'), may hold values from -0.125 to 0.125
- shared_w_up: bfloat16 [2048, 2816], P(None, 'tp'), may hold values from -0.125 to 0.125
- shared_w_down: bfloat16 [2816, 2048], P('tp'), may hold values from -0.109375 to 0.109375
Outputs:
- moe_out: bfloat16 [2048, 2048], P('ep', 'tp')
Inputs may be any that keep to these rules, and one draw needn't show every extreme that they name: `expert_ids`: each row names 4 different experts below 60. Within the 256 rows of one index of ep no expert is named by more than 32 rows, and in some of these blocks one expert is named by exactly 32 rows.
All inputs are finite; a program needn't handle non-finite values.
Results may differ from a plain program's by a relative error of at most 0.0069.
Values may be sent and summed in bfloat16 or wider, within the bound.
A program may use at most 128 MiB of HBM per device.

v0:
```python
import jax
import jax.numpy as jnp
from jax import lax
from jax.sharding import PartitionSpec as P

F32 = jnp.float32
BF16 = jnp.bfloat16


def send_back(summed):
    return lax.all_to_all(summed, "ep", split_axis=0, concat_axis=0, tiled=True)


def expert_rows(arrived, w_gate, w_up, w_down):
    gate_act = jnp.einsum("sekd,edf->sekf", arrived, w_gate, preferred_element_type=jnp.float32)
    up_act = jnp.einsum("sekd,edf->sekf", arrived, w_up, preferred_element_type=jnp.float32)
    hidden = (jax.nn.silu(gate_act) * up_act).astype(jnp.bfloat16)
    partial_out = jnp.einsum("sekf,efd->sekd", hidden, w_down, preferred_element_type=jnp.float32)
    summed = lax.psum_scatter(partial_out, "tp", scatter_dimension=3, tiled=True).astype(
        jnp.bfloat16
    )
    return send_back(summed)


def sliced_rows(arrived, w_gate, w_up, w_down):
    complete = lax.all_gather(arrived, "tp", axis=3, tiled=True)
    return expert_rows(complete, w_gate, w_up, w_down)


def dispatch_plan(
    tokens,
    norm_gain,
    router_weight,
    shared_gate_w,
    expert_ids,
    w_gate,
    w_up,
    w_down,
    shared_w_gate,
    shared_w_up,
    shared_w_down,
):
    width = tokens.shape[1]
    tok_rows = tokens.shape[0]
    column_start = lax.axis_index("tp") * width
    whole = lax.all_gather(tokens, "tp", axis=1, tiled=True)
    values = whole.astype(jnp.float32)
    inv_rms = lax.rsqrt(jnp.mean(values * values, axis=-1, keepdims=True) + 1e-06)
    normed = (values * inv_rms * norm_gain[None, :]).astype(jnp.bfloat16)
    own_part = lax.dynamic_slice_in_dim(normed, column_start, width, 1)
    partial_logits = jnp.dot(own_part, router_weight, preferred_element_type=jnp.float32)
    logits = lax.psum(partial_logits, "tp")
    probs = jax.nn.softmax(logits, axis=-1)
    expert_count = logits.shape[1]
    matches = expert_ids[:, :, None] == jnp.arange(expert_count, dtype=jnp.int32)[None, None, :]
    route_weight = jnp.sum(jnp.where(matches, probs[:, None, :], 0.0), axis=-1)
    gate_whole, up_whole, down_whole = (w_gate, w_up, w_down)
    experts_here = w_gate.shape[0]
    slot_count = lax.axis_size("ep") * experts_here
    capacity = tok_rows // 8
    flat_ids = expert_ids.reshape(-1)
    one_hot = (flat_ids[:, None] == jnp.arange(slot_count, dtype=jnp.int32)[None, :]).astype(
        jnp.int32
    )
    before = jnp.cumsum(one_hot, axis=0) - one_hot
    order_rank = jnp.sum(before * one_hot, axis=1)
    slot_ids = (flat_ids * capacity + order_rank).reshape(expert_ids.shape)
    targets = jnp.arange(slot_count * capacity, dtype=jnp.int32)
    dispatch_map = jnp.sum(
        (slot_ids[None, :, :] == targets[:, None, None]).astype(jnp.bfloat16), axis=2
    )
    outgoing = jnp.dot(dispatch_map, own_part, preferred_element_type=jnp.float32).astype(
        jnp.bfloat16
    )
    outgoing = outgoing.reshape(lax.axis_size("ep"), experts_here, capacity, width)
    returned = sliced_rows(
        lax.all_to_all(outgoing, "ep", split_axis=0, concat_axis=0, tiled=True),
        w_gate=gate_whole,
        w_up=up_whole,
        w_down=down_whole,
    )
    picked = returned.reshape(slot_count * capacity, width)[slot_ids]
    routed = jnp.sum(route_weight[:, :, None] * picked.astype(jnp.float32), axis=1)
    shared_gate_act = jnp.dot(normed, shared_w_gate, preferred_element_type=jnp.float32)
    shared_up_act = jnp.dot(normed, shared_w_up, preferred_element_type=jnp.float32)
    shared_hidden = (jax.nn.silu(shared_gate_act) * shared_up_act).astype(jnp.bfloat16)
    shared_part = jnp.dot(shared_hidden, shared_w_down, preferred_element_type=jnp.float32)
    shared_own = lax.psum_scatter(shared_part, "tp", scatter_dimension=1, tiled=True)
    share_gate = jax.nn.sigmoid(jnp.dot(normed, shared_gate_w, preferred_element_type=jnp.float32))
    return (share_gate[:, None] * shared_own + routed).astype(jnp.bfloat16)


def gather_plan(
    tokens,
    norm_gain,
    router_weight,
    shared_gate_w,
    expert_ids,
    w_gate,
    w_up,
    w_down,
    shared_w_gate,
    shared_w_up,
    shared_w_down,
):
    rows, width = tokens.shape
    n_ep = lax.axis_size("ep")
    n_tp = lax.axis_size("tp")
    full = n_tp * width
    here = w_gate.shape[0]
    cap = rows // 8
    me = lax.axis_index("ep")

    every = lax.all_gather(tokens, ("ep", "tp"), axis=0)
    ids = lax.all_gather(expert_ids.reshape(-1), "ep", axis=0)
    ids = ids.reshape(n_ep, rows, expert_ids.shape[1])
    router = lax.all_gather(router_weight, "tp", axis=0, tiled=True)

    whole = every.reshape(n_ep, n_tp, rows, width).transpose(0, 2, 1, 3)
    values = whole.reshape(n_ep, rows, full).astype(F32)
    inv_rms = lax.rsqrt(jnp.mean(values * values, axis=-1, keepdims=True) + 1e-06)
    normed = (values * inv_rms * norm_gain).astype(BF16)

    logits = jnp.einsum("std,dx->stx", normed, router, preferred_element_type=F32)
    probs = jax.nn.softmax(logits, axis=-1)
    probs = jnp.pad(probs, ((0, 0), (0, 0), (0, n_ep * here - probs.shape[-1])))
    local = lax.dynamic_slice_in_dim(probs, me * here, here, 2)
    names = me * here + jnp.arange(here, dtype=jnp.int32)
    match = jnp.any(ids[:, :, :, None] == names, axis=2)
    lower = jnp.tril(jnp.ones((rows, rows), BF16), -1)
    rank = jnp.einsum("tu,suj->sjt", lower, match.astype(BF16), preferred_element_type=F32)
    match_t = match.transpose(0, 2, 1)
    spot = jnp.where(match_t, rank, -1.0).astype(jnp.int32)
    pick = spot[:, :, None, :] == jnp.arange(cap, dtype=jnp.int32)[None, None, :, None]
    slot_w = jnp.sum(jnp.where(pick, local.transpose(0, 2, 1)[:, :, None, :], 0.0), axis=-1)
    pick = pick.astype(BF16)

    x = jnp.einsum("sjkt,std->jskd", pick, normed, preferred_element_type=F32).astype(BF16)
    gate = jnp.einsum("jskd,jdf->jskf", x, w_gate, preferred_element_type=F32)
    up = jnp.einsum("jskd,jdf->jskf", x, w_up, preferred_element_type=F32)
    hidden = (jax.nn.silu(gate) * up).astype(BF16)
    y = jnp.einsum("jskf,jfd->jskd", hidden, w_down, preferred_element_type=F32)
    y = (y * slot_w.transpose(1, 0, 2)[..., None]).astype(BF16)
    routed = jnp.einsum("sjkt,jskd->std", pick, y, preferred_element_type=F32)

    own = lax.dynamic_index_in_dim(normed, me, 0, keepdims=False)
    sg = jnp.dot(own, shared_w_gate, preferred_element_type=F32)
    su = jnp.dot(own, shared_w_up, preferred_element_type=F32)
    sh = (jax.nn.silu(sg) * su).astype(BF16)
    part = jnp.dot(sh, shared_w_down, preferred_element_type=F32)
    share = jax.nn.sigmoid(jnp.dot(own, shared_gate_w, preferred_element_type=F32))
    part = share[:, None] * part
    mine = (jnp.arange(n_ep) == me)[:, None, None]
    total = (routed + jnp.where(mine, part[None], 0.0)).astype(BF16)
    total = total.reshape(n_ep, rows, n_tp, width)
    total = lax.psum_scatter(total, "tp", scatter_dimension=2, tiled=True)
    total = total.reshape(n_ep * rows, width)
    terms = lax.all_to_all(total, "ep", split_axis=0, concat_axis=0, tiled=True)
    return jnp.sum(terms.reshape(n_ep, rows, width).astype(F32), axis=0).astype(BF16)


def solution(mesh):
    def per_device(tokens, *rest):
        gathered = mesh.size * tokens.size * tokens.dtype.itemsize
        plan = gather_plan if gathered <= 16 << 20 else dispatch_plan
        return plan(tokens, *rest)

    return jax.shard_map(
        per_device,
        mesh=mesh,
        in_specs=(
            P("ep", "tp"),
            P(),
            P("tp", None),
            P(),
            P("ep", None),
            P("ep", None, "tp"),
            P("ep", None, "tp"),
            P("ep", "tp", None),
            P(None, "tp"),
            P(None, "tp"),
            P("tp", None),
        ),
        out_specs=P("ep", "tp"),
        check_vma=False,
    )
```

profile of v0, /device:TPU:0, one launch (start us, length us, event | category | flops | bytes accessed | tf_op | source)
XLA Modules:
  0.0 321.4 jit_solution(6861962941490669970)
XLA Ops:
  6.5 0.7 all-gather.4.cloned.1.call-update
  7.3 0.8 reshape.64
  8.1 0.8 copy.36
  9.0 32.6 %all-gather.1 = s32[8,1,1024]{2,1,0:T(1,128)S(1)} all-gather(s32[1,1,1024]{2,1,0:T(1,128)S(1)} %reshape.53), channel_id=1, replica_groups=mesh['ep'=8,'tp'=4] {'ep'}, dimensions={0}, use_global_device_ids=true | all-gather | bytes 36864 | tf_op jit(solution)/shard_map/all_gather | solution.py:115
  42.0 7.4 %all_gather.15 = bf16[2048,60]{0,1:T(8,128)(2,1)} all-gather(bf16[512,60]{0,1:T(8,128)(2,1)} %param.13), channel_id=1, replica_groups=mesh['ep'=8,'tp'=4] {'tp'}, dimensions={0}, use_global_device_ids=true | all-gather | bytes 307200 | tf_op jit(solution)/shard_map/all_gather | solution.py:117
  49.6 0.3 fusion.29
  49.8 40.2 %all-gather.4.cloned.1.call-done = bf16[8192,512]{1,0:T(8,128)(2,1)} async-done(((bf16[256,512]{1,0:T(8,128)(2,1)}), bf16[8192,512]{1,0:T(8,128)(2,1)}) %all-gather.4.cloned.1.call-update) | async-done | bytes 8388624 | tf_op jit(solution)/shard_map/all_gather | solution.py:114
  90.1 11.5 %copy.51 = f32[8,4,32,8,512]{4,3,1,2,0:T(8,128)} copy(bf16[8,4,32,8,512]{4,3,2,1,0:T(8,128)(2,1)} %bitcast.78) | data formatting | bytes 25165824 | tf_op jit(solution)/shard_map/convert_element_type | solution.py:120
  101.6 5.1 %multiply_reduce_fusion = f32[8192]{0:T(1024)S(1)} fusion(bf16[8192,512]{1,0:T(8,128)(2,1)} %all-gather.4.cloned.1.call-done), kind=kLoop, calls=%fused_computation.3 | loop fusion | flops 12574720 | bytes 8421376 | tf_op jit(solution)/shard_map/reduce_sum | solution.py:121
  106.8 7.1 %multiply_convert_fusion.1 = bf16[8,256,2048]{2,1,0:T(8,128)(2,1)S(1)} fusion(f32[8,256,2048]{2,1,0:T(8,128)} %bitcast.77, f32[2048]{0:T(1024)S(1)} %copy-done.3, f32[8,256]{1,0:T(8,128)S(1)} %add_rsqrt_fusion), kind=kLoop, calls=%fused_computation.5 | loop fusion | flops 12582912 | bytes 25182208 | tf_op jit(solution)/shard_map/convert_element_type | solution.py:122
  114.0 2.3 fusion.31
  116.3 1.1 copy-done.2
  117.4 0.4 fusion.33
  117.8 6.1 %fusion.51 = f32[8,256,60]{1,2,0:T(8,128)S(1)} fusion(bf16[8,256,2048]{2,1,0:T(8,128)(2,1)} %copy-done.2, bf16[2048,60]{0,1:T(8,128)(2,1)} %all_gather.15), kind=kOutput, calls=%fused_computation.51 | convolution fusion | flops 503566464 | bytes 9125888 | tf_op jit(solution)/shard_map/div | solution.py:125
  123.9 8.9 %convert_bitcast_fusion = bf16[8,8,32,2048]{3,2,0,1:T(8,128)(2,1)} fusion(bf16[8,256,2048]{2,1,0:T(8,128)(2,1)} %copy-done.2, s32[8,8,256]{2,1,0:T(8,128)S(1)} %fusion.29), kind=kOutput, calls=%fused_computation.17 | convolution fusion | flops 2152202240 | bytes 16842752 | tf_op jit(solution)/shard_map/sjkt,std->jskd/dot_general | solution.py:138
  132.9 0.4 select_reduce_fusion
  133.3 12.8 %fusion.4 = f32[8,8,32,352]{3,2,1,0:T(8,128)} fusion(bf16[8,2048,352]{1,2,0:T(8,128)(2,1)} %param.16, bf16[8,8,32,2048]{3,2,0,1:T(8,128)(2,1)} %convert_bitcast_fusion), kind=kOutput, calls=%fused_computation.8 | convolution fusion | flops 2952790016 | bytes 22806528 | tf_op jit(solution)/shard_map/jskd,jdf->jskf/dot_general | solution.py:139
  146.1 14.6 %multiply_convert_fusion.3 = bf16[8,8,32,352]{3,2,1,0:T(8,128)(2,1)} fusion(f32[8,8,32,352]{3,2,1,0:T(8,128)} %fusion.4, bf16[8,2048,352]{1,2,0:T(8,128)(2,1)} %param.17, bf16[8,8,32,2048]{3,2,0,1:T(8,128)(2,1)} %convert_bitcast_fusion), kind=kOutput, calls=%fused_computation.20 | convolution fusion | flops 2957115392 | bytes 24248320 | tf_op jit(solution)/shard_map/jskd,jdf->jskf/dot_general | solution.py:140
  160.7 7.0 %convolution_multiply_fusion = f32[256,2048]{1,0:T(8,128)} fusion(bf16[704,2048]{1,0:T(8,128)(2,1)S(1)} %copy-done, f32[256]{0:T(256)S(1)} %add_divide_fusion, bf16[2048,704]{0,1:T(8,128)(2,1)} %param.20, bf16[8,256,2048]{2,1,0:T(8,128)(2,1)} %copy-done.2, s32[]{:T(128)S(6)} %select_n.27, f32[256,704]{0,1:T(8,128)} %fusion.31), kind=kOutput, calls=%fused_computation.21 | convolution fusion | flops 1478000640 | bytes 9634820 | tf_op jit(solution)/shard_map/dot_general | solution.py:150
  167.6 12.5 %fusion.1 = bf16[8,256,2048]{2,1,0:T(8,128)(2,1)} fusion(f32[256,2048]{1,0:T(8,128)} %convolution_multiply_fusion, pred[8]{0:T(512)(128)(4,1)S(1)} %iota_compare_fusion.4, f32[8,8,32]{2,0,1:T(8,128)S(1)} %bitcast.82, bf16[8,352,2048]{2,1,0:T(8,128)(2,1)} %param.18, bf16[8,8,32,352]{3,2,1,0:T(8,128)(2,1)} %multiply_convert_fusion.3, s32[8,8,256]{2,1,0:T(8,128)S(1)} %fusion.29), kind=kOutput, calls=%fused_computation.2 | convolution fusion | flops 5121769472 | bytes 23535624 | tf_op jit(solution)/shard_map/sjkt,jskd->std/dot_general | solution.py:144
  180.1 7.9 %copy.62 = bf16[8,32,4,8,512]{4,3,1,0,2:T(8,128)(2,1)} copy(bf16[8,32,4,8,512]{4,3,2,1,0:T(8,128)(2,1)} %bitcast.76) | data formatting | bytes 16777216 | tf_op jit(solution)/shard_map/reshape | solution.py:155
  188.0 70.2 %reduce-scatter.2.cloned.1.call-done = bf16[8,256,1,512]{3,1,0,2:T(8,128)(2,1)} async-done(((bf16[8,256,4,512]{3,1,0,2:T(8,128)(2,1)}), bf16[8,256,1,512]{3,1,0,2:T(8,128)(2,1)}) %reduce-scatter.2.cloned.1.call-update) | async-done | bytes 2097168 | tf_op jit(solution)/shard_map/reduce_scatter | solution.py:156
  258.2 53.7 %all_to_all.9 = bf16[8,256,512]{2,1,0:T(8,128)(2,1)} all-to-all(bf16[8,256,512]{2,1,0:T(8,128)(2,1)} %bitcast.80), channel_id=1, replica_groups=mesh['ep'=8,'tp'=4] {'ep'}, dimensions={0} | all-to-all | bytes 4194304 | tf_op jit(solution)/shard_map/all_to_all | solution.py:158
  311.9 2.7 reduce_sum.51
  (24 shorter events, 0.8 us)
Async XLA Ops:
  6.5 154.1 %copy-start = (bf16[704,2048]{1,0:T(8,128)(2,1)S(1)}, bf16[704,2048]{1,0:T(8,128)(2,1)}, u32[]{:S(2)}) copy-start(bf16[704,2048]{1,0:T(8,128)(2,1)} %param.21) | copy-start | bytes 8650756
  6.5 83.5 %all-gather.4.cloned.1.call-start = ((), (), s32[]{:S(2)}) async-start(), calls=%async_computation.3 | async-start | bytes 8650752 | tf_op jit(solution)/shard_map/all_gather | solution.py:114
  7.3 250.9 %reduce-scatter.2.cloned.1.call-start = ((), (), s32[]{:S(2)}) async-start(), calls=%async_computation.2 | async-start | bytes 10485760 | tf_op jit(solution)/shard_map/reduce_scatter | solution.py:156
  101.6 5.2 %copy-start.3 = (f32[2048]{0:T(1024)S(1)}, f32[2048]{0:T(1024)}, u32[]{:S(2)}) copy-start(f32[2048]{0:T(1024)} %param.12) | copy-start | bytes 24580
  106.8 7.1 %copy-start.4 = (bf16[2048,704]{0,1:T(8,128)(2,1)S(1)}, bf16[2048,704]{0,1:T(8,128)(2,1)}, u32[]{:S(2)}) copy-start(bf16[2048,704]{0,1:T(8,128)(2,1)} %param.19) | copy-start | bytes 8650756
  114.0 3.4 %copy-start.2 = (bf16[8,256,2048]{2,1,0:T(8,128)(2,1)}, bf16[8,256,2048]{2,1,0:T(8,128)(2,1)S(1)}, u32[]{:S(2)}) copy-start(bf16[8,256,2048]{2,1,0:T(8,128)(2,1)S(1)} %multiply_convert_fusion.1) | copy-start | bytes 25165828
  180.1 134.4 %copy-start.1 = (bf16[704,2048]{1,0:T(8,128)(2,1)S(1)}, bf16[704,2048]{1,0:T(8,128)(2,1)}, u32[]{:S(2)}) copy-start(bf16[704,2048]{1,0:T(8,128)(2,1)} %param.21) | copy-start | bytes 8650756
Sparse Core Ops, SparseCore 0:
  10.2 79.8 all-gather.3
  188.1 70.0 reduce-scatter.1
where the time goes:
time: 322 us; the launch traced here: 321 us
  waiting for transfers between devices  111 us (34%)
  blocking collectives  93.7 us (29%)
  matrix products  64.8 us (20%)
  local copies, waits for them, and re-layouts  22.7 us (7%)
  other arithmetic  15.5 us (5%)
  between operations  13.5 us (4%)
    reduce_scatter x1, waiting for transfers between devices, gather_plan(): total = lax.psum_scatter(total, 'tp', scatter_dimension=2, tiled=True)  70.2 us
    all_to_all x1, blocking collectives, gather_plan(): terms = lax.all_to_all(total, 'ep', split_axis=0, concat_axis=0, tiled=True)  53.7 us
    all_gather x1, waiting for transfers between devices, gather_plan(): every = lax.all_gather(tokens, ('ep', 'tp'), axis=0)  40.2 us
    all_gather x1, blocking collectives, gather_plan(): ids = lax.all_gather(expert_ids.reshape(-1), 'ep', axis=0)  32.6 us
    dot_general x1, matrix products, gather_plan(): up = jnp.einsum('jskd,jdf->jskf', x, w_up, preferred_element_type=F32)  14.6 us
    dot_general x1, matrix products, gather_plan(): gate = jnp.einsum('jskd,jdf->jskf', x, w_gate, preferred_element_type=F32)  12.8 us
    dot_general x1, matrix products, gather_plan(): routed = jnp.einsum('sjkt,jskd->std', pick, y, preferred_element_type=F32)  12.5 us
    convert_element_type x1, local copies, waits for them, and re-layouts, gather_plan(): values = whole.reshape(n_ep, rows, full).astype(F32)  11.5 us
  transfers between devices with their start and end apart: 2, of which 2 were waited for; matrix products, arithmetic and copies ran while one was open for 1% of the time, Pallas kernels for 0%

commit v1 on v0

--- a/solution.py
+++ b/solution.py
@@ -1,10 +1,424 @@
+import functools
+
 import jax
 import jax.numpy as jnp
 from jax import lax
+from jax.experimental import pallas as pl
+from jax.experimental.pallas import tpu as pltpu
 from jax.sharding import PartitionSpec as P
 
 F32 = jnp.float32
 BF16 = jnp.bfloat16
+MESH = pl.DeviceIdType.MESH
+
+
+def offsets(nz, order):
+    span = {"z": range(-(nz - 1), nz), "x": (0, 1), "y": (0, 1)}
+    take = lambda d: span[d] if d in order else (0,)
+    return [(a, b, c) for a in take("z") for b in take("x") for c in take("y")]
+
+
+def last_dim(order, off):
+    value = dict(zip("zxy", off))
+    return max([i for i, d in enumerate(order) if value[d] != 0], default=-1)
+
+
+def next_hops(order, off, nz):
+    last, dz = last_dim(order, off), off[0]
+    hops = []
+    for i, d in enumerate(order):
+        if d == "z":
+            if (last < i or (last == i and dz > 0)) and dz < nz - 1:
+                hops.append("u")
+            if (last < i or (last == i and dz < 0)) and dz > 1 - nz:
+                hops.append("d")
+        elif last < i:
+            hops.append(d)
+    return hops
+
+
+def moved(off, hop):
+    dz, dx, dy = off
+    return {
+        "u": (dz + 1, dx, dy),
+        "d": (dz - 1, dx, dy),
+        "x": (dz, 1 - dx, dy),
+        "y": (dz, dx, 1 - dy),
+    }[hop]
+
+
+def event_order(nz, streams):
+    events = []
+    for k, (order, _, n) in enumerate(streams):
+        for off in offsets(nz, order):
+            value = {"z": abs(off[0]), "x": off[1], "y": off[2]}
+            when, load = 0.0, 1
+            for d in order:
+                when += value[d] * load * n
+                load *= nz if d == "z" else 2
+            events.append((when, k, off))
+    events.sort()
+    return [(k, off) for _, k, off in events]
+
+
+def block_streams(rows):
+    part = rows // 16
+    cuts = (("zxy", 3 * part), ("zyx", 3 * part), ("xzy", 5 * part), ("yzx", 5 * part))
+    streams, start = [], 0
+    for order, n in cuts:
+        streams.append((order, start, n))
+        start += n
+    return streams
+
+
+class Plan:
+    def __init__(self, n_ep, rows):
+        self.nz = n_ep // 2
+        self.streams = block_streams(rows)
+        self.extra = [("zx", 0, 1), ("y", 0, 1)]
+        every = self.extra + self.streams
+        self.events = event_order(self.nz, every)
+        self.sends, self.recvs, self.pair = {}, {}, {}
+        for k, off in self.events:
+            for hop in next_hops(every[k][0], off, self.nz):
+                self.sends[k, off, hop] = len(self.sends)
+            self.recvs[k, off] = len(self.recvs)
+            if k != 0:
+                self.pair[k, off] = len(self.pair)
+        self.every = every
+        self.back = [(k, off) for k, off in reversed(self.events) if k >= 2]
+        self.slots, self.slot_rows = {}, 0
+        for k, off in self.back:
+            for hop in next_hops(every[k][0], off, self.nz):
+                self.slots[k, off, hop] = (len(self.slots), self.slot_rows)
+                self.slot_rows += every[k][2]
+        self.parents = {e: i for i, e in enumerate(self.back)}
+
+
+def kernel(plan, n_tp, here, experts,
+           tok, gain, sgw, rt, ids, wg, wu, wd, swg, swu, swd, out,
+           g, xs, pick, sw, pr, part, rbuf, idb, wgb, wub, wdb, sgb, sub, sdb, slot, cbuf,
+           loc, wsem, ssem, send, recv, psend, precv, bsend, brecv, bpsend, bprecv):
+    nz = plan.nz
+    ep, tp = lax.axis_index("ep"), lax.axis_index("tp")
+    z, x, y, c = ep // 2, ep % 2, tp // 2, tp % 2
+    rows, width = tok.shape
+    n_ep = 2 * nz
+    cap = rows // 8
+
+    def dev(z_, x_, y_, c_):
+        return (z_ * 2 + x_, y_ * 2 + c_)
+
+    to = {
+        "u": dev(z + 1, x, y, c),
+        "d": dev(z - 1, x, y, c),
+        "x": dev(z, 1 - x, y, c),
+        "y": dev(z, x, 1 - y, c),
+        "c": dev(z, x, y, 1 - c),
+    }
+    exists = {"u": z < nz - 1, "d": z > 0}
+
+    def when(conds, body):
+        if not conds:
+            body()
+            return
+        cond = conds[0]
+        for other in conds[1:]:
+            cond = jnp.logical_and(cond, other)
+        pl.when(cond)(body)
+
+    barrier = pltpu.get_barrier_semaphore()
+    for hop in to:
+        when([exists[hop]] if hop in exists else [],
+             lambda hop=hop: pl.semaphore_signal(barrier, inc=1, device_id=to[hop], device_id_type=MESH))
+
+    own = [
+        pltpu.make_async_copy(tok, g.at[ep, tp], loc.at[0]),
+        pltpu.make_async_copy(ids, idb.at[ep], loc.at[1]),
+        pltpu.make_async_copy(rt, rbuf.at[tp], loc.at[2]),
+    ]
+    for cp in own:
+        cp.start()
+    shared_copies = [
+        pltpu.make_async_copy(a, b, ssem.at[i]) for i, (a, b) in enumerate(((swg, sgb), (swu, sub), (swd, sdb)))
+    ]
+
+    def weights(j, buf):
+        return [
+            pltpu.make_async_copy(a.at[j], b.at[buf], wsem.at[i, buf])
+            for i, (a, b) in enumerate(((wg, wgb), (wu, wub), (wd, wdb)))
+        ]
+
+    for cp in shared_copies + weights(0, 0) + weights(1, 1):
+        cp.start()
+    pl.semaphore_wait(barrier, 3 + jnp.where(exists["u"], 1, 0) + jnp.where(exists["d"], 1, 0))
+    for cp in own:
+        cp.wait()
+
+    def place(k, off, core):
+        zs, xx, yy = z - off[0], (x + off[1]) % 2, (y + off[2]) % 2
+        e, t = zs * 2 + xx, yy * 2 + core
+        if k == 0:
+            return idb.at[e]
+        if k == 1:
+            return rbuf.at[t]
+        _, start, n = plan.every[k]
+        return g.at[e, t, pl.ds(start, n), :]
+
+    def valid(off):
+        if off[0] > 0:
+            return [z >= off[0]]
+        if off[0] < 0:
+            return [z < nz + off[0]]
+        return []
+
+    def hop_copy(k, off, hop):
+        ref = place(k, off, c)
+        return pltpu.make_async_remote_copy(
+            src_ref=ref, dst_ref=ref,
+            send_sem=send.at[plan.sends[k, off, hop]],
+            recv_sem=recv.at[plan.recvs[k, moved(off, hop)]],
+            device_id=to[hop], device_id_type=MESH)
+
+    def arrival(k, off):
+        ref = place(k, off, c)
+        return pltpu.make_async_remote_copy(
+            src_ref=ref, dst_ref=ref, send_sem=send.at[0], recv_sem=recv.at[plan.recvs[k, off]],
+            device_id=to["c"], device_id_type=MESH)
+
+    def pair_copy(k, off, core):
+        ref = place(k, off, core)
+        i = plan.pair[k, off]
+        return pltpu.make_async_remote_copy(
+            src_ref=ref, dst_ref=ref, send_sem=psend.at[i], recv_sem=precv.at[i],
+            device_id=to["c"], device_id_type=MESH)
+
+    for k, off in plan.events:
+        order = plan.every[k][0]
+
+        def step(k=k, off=off, order=order):
+            if off != (0, 0, 0):
+                arrival(k, off).wait_recv()
+            for hop in next_hops(order, off, nz):
+                when([exists[hop]] if hop in exists else [], lambda: hop_copy(k, off, hop).start())
+            if k != 0:
+                pair_copy(k, off, c).start()
+
+        when(valid(off), step)
+
+    def finish(k, off):
+        for hop in next_hops(plan.every[k][0], off, nz):
+            when([exists[hop]] if hop in exists else [], lambda: hop_copy(k, off, hop).wait_send())
+        if k != 0:
+            pair_copy(k, off, 1 - c).wait_recv()
+            pair_copy(k, off, c).wait_send()
+
+    for k, off in plan.events:
+        when(valid(off), lambda k=k, off=off: finish(k, off))
+
+    slots = n_ep * here
+
+    @pl.loop(0, n_ep)
+    def _(s):
+        total = jnp.zeros((rows, 1), F32)
+        for t in range(n_tp):
+            v = g[s, t].astype(F32)
+            total = total + jnp.sum(v * v, axis=-1, keepdims=True)
+        inv = lax.rsqrt(total / (n_tp * width) + 1e-6)
+        logits = jnp.zeros((slots, rows), F32)
+        for t in range(n_tp):
+            v = g[s, t].astype(F32) * inv * gain[:, t * width:(t + 1) * width]
+            v = v.astype(BF16)
+            g[s, t] = v
+            logits = logits + lax.dot_general(rbuf[t], v, (((1,), (1,)), ((), ())), preferred_element_type=F32)
+        names = lax.broadcasted_iota(jnp.int32, (slots, rows), 0)
+        logits = jnp.where(names < experts, logits, -1e30)
+        ex = jnp.exp(logits - jnp.max(logits, axis=0, keepdims=True))
+        ex = jnp.where(names < experts, ex, 0.0)
+        pr[...] = ex / jnp.sum(ex, axis=0, keepdims=True)
+        probs = pr[pl.ds(pl.multiple_of(ep * here, here), here), :]
+        mine = ep * here + lax.broadcasted_iota(jnp.int32, (here, rows), 0)
+        match = jnp.zeros((here, rows), jnp.bool_)
+        for q in range(ids.shape[0]):
+            match = jnp.logical_or(match, mine == idb[s, q:q + 1, :])
+        hit = jnp.where(match, 1.0, 0.0)
+        upper = jnp.where(
+            lax.broadcasted_iota(jnp.int32, (rows, rows), 0) < lax.broadcasted_iota(jnp.int32, (rows, rows), 1), 1.0, 0.0)
+        rank = jnp.dot(hit.astype(BF16), upper.astype(BF16), preferred_element_type=F32)
+        spot = jnp.where(match, rank, -1.0).astype(jnp.int32)
+        spots = lax.broadcasted_iota(jnp.int32, (cap, rows), 0)
+        for j in range(here):
+            one = spot[j:j + 1, :] == spots
+            sw[j, pl.ds(pl.multiple_of(s * cap, cap), cap), :] = jnp.sum(
+                jnp.where(one, probs[j:j + 1, :], 0.0), axis=1, keepdims=True)
+            pick[s, j * cap:(j + 1) * cap, :] = jnp.where(one, 1.0, 0.0).astype(BF16)
+        for t in range(n_tp):
+            v = jnp.dot(pick[s], g[s, t], preferred_element_type=F32).astype(BF16)
+            for j in range(here):
+                xs[j, pl.ds(pl.multiple_of(s * cap, cap), cap), t * width:(t + 1) * width] = v[j * cap:(j + 1) * cap]
+
+    for cp in shared_copies:
+        cp.wait()
+    sg = jnp.zeros((rows, sgb.shape[1]), F32)
+    su = jnp.zeros((rows, sgb.shape[1]), F32)
+    gate = jnp.zeros((rows, 1), F32)
+    for t in range(n_tp):
+        v = g[ep, t]
+        sg = sg + jnp.dot(v, sgb[t * width:(t + 1) * width, :], preferred_element_type=F32)
+        su = su + jnp.dot(v, sub[t * width:(t + 1) * width, :], preferred_element_type=F32)
+        gate = gate + jnp.sum(v.astype(F32) * sgw[:, t * width:(t + 1) * width].astype(F32), axis=-1, keepdims=True)
+    sh = (sg / (1.0 + jnp.exp(-sg)) * su).astype(BF16)
+    gate = 1.0 / (1.0 + jnp.exp(-gate))
+    for t in range(n_tp):
+        part[t] = gate * jnp.dot(sh, sdb[:, t * width:(t + 1) * width], preferred_element_type=F32)
+
+    @pl.loop(0, here)
+    def _(j):
+        buf = j % 2
+        for cp in weights(j, buf):
+            cp.wait()
+        v = xs[j]
+        a = jnp.dot(v, wgb[buf], preferred_element_type=F32)
+        b = jnp.dot(v, wub[buf], preferred_element_type=F32)
+        h = (a / (1.0 + jnp.exp(-a)) * b).astype(BF16)
+        for t in range(n_tp):
+            o = jnp.dot(h, wdb[buf, :, t * width:(t + 1) * width], preferred_element_type=F32)
+            xs[j, :, t * width:(t + 1) * width] = (o * sw[j]).astype(BF16)
+
+        @pl.when(j + 2 < here)
+        def _():
+            for cp in weights(j + 2, buf):
+                cp.start()
+
+    @pl.loop(0, n_ep)
+    def _(s):
+        for t in range(n_tp):
+            v = xs[:, pl.ds(pl.multiple_of(s * cap, cap), cap), t * width:(t + 1) * width]
+            v = v.reshape(here * cap, width)
+            o = lax.dot_general(pick[s], v, (((0,), (0,)), ((), ())), preferred_element_type=F32)
+            o = o + jnp.where(s == ep, part[t], 0.0)
+            g[s, t] = o.astype(BF16)
+
+    def pair_back(k, off, core):
+        ref = place(k, off, core)
+        zs, xx, yy = z - off[0], (x + off[1]) % 2, (y + off[2]) % 2
+        _, start, n = plan.every[k]
+        i = plan.parents[k, off]
+        return pltpu.make_async_remote_copy(
+            src_ref=ref, dst_ref=cbuf.at[zs * 2 + xx, yy, pl.ds(start, n), :],
+            send_sem=bpsend.at[i], recv_sem=bprecv.at[i], device_id=to["c"], device_id_type=MESH)
+
+    def child_copy(k, off, hop):
+        i, start = plan.slots[k, off, hop]
+        ref = slot.at[pl.ds(start, plan.every[k][2]), :]
+        return pltpu.make_async_remote_copy(
+            src_ref=ref, dst_ref=ref, send_sem=bsend.at[0], recv_sem=brecv.at[i],
+            device_id=to["c"], device_id_type=MESH), ref
+
+    def parent(k, off):
+        order = plan.every[k][0]
+        d = order[last_dim(order, off)]
+        if d == "z":
+            hop = "d" if off[0] > 0 else "u"
+            seen = "u" if off[0] > 0 else "d"
+        else:
+            hop = seen = d
+        up = moved(off, hop)
+        i, start = plan.slots[k, up, seen]
+        return pltpu.make_async_remote_copy(
+            src_ref=place(k, off, c), dst_ref=slot.at[pl.ds(start, plan.every[k][2]), :],
+            send_sem=bsend.at[plan.parents[k, off]], recv_sem=brecv.at[i],
+            device_id=to[hop], device_id_type=MESH)
+
+    for k, off in plan.back:
+        when(valid(off), lambda k=k, off=off: pair_back(k, off, 1 - c).start())
+    for k, off in plan.back:
+        def step(k=k, off=off):
+            _, start, n = plan.every[k]
+            zs, xx, yy = z - off[0], (x + off[1]) % 2, (y + off[2]) % 2
+            pair_back(k, off, c).wait_recv()
+            mine = place(k, off, c)
+            acc = mine[...].astype(F32) + cbuf[zs * 2 + xx, yy, start:start + n, :].astype(F32)
+            for hop in next_hops(plan.every[k][0], off, nz):
+                cp, ref = child_copy(k, off, hop)
+                if hop in exists:
+                    pl.when(exists[hop])(lambda cp=cp: cp.wait_recv())
+                    acc = acc + jnp.where(exists[hop], ref[...].astype(F32), 0.0)
+                else:
+                    cp.wait_recv()
+                    acc = acc + ref[...].astype(F32)
+            if off == (0, 0, 0):
+                out[start:start + n, :] = acc.astype(BF16)
+            else:
+                mine[...] = acc.astype(BF16)
+                parent(k, off).start()
+        when(valid(off), step)
+    for k, off in plan.back:
+        def done(k=k, off=off):
+            pair_back(k, off, 1 - c).wait_send()
+            if off != (0, 0, 0):
+                parent(k, off).wait_send()
+        when(valid(off), done)
+
+
+def fused_plan(mesh, tokens, norm_gain, router_weight, shared_gate_w, expert_ids, w_gate, w_up, w_down,
+               shared_w_gate, shared_w_up, shared_w_down):
+    rows, width = tokens.shape
+    n_ep, n_tp = mesh.shape["ep"], mesh.shape["tp"]
+    here, full, hid = w_gate.shape
+    experts = router_weight.shape[1]
+    shid = shared_w_gate.shape[1]
+    slots, cap = n_ep * here, rows // 8
+    plan = Plan(n_ep, rows)
+    rt = jnp.pad(router_weight.T, ((0, slots - experts), (0, 0)))
+    ids = jnp.pad(expert_ids.T, ((0, -expert_ids.shape[1] % 8), (0, 0)), constant_values=-1)
+    vmem, hbm = pl.BlockSpec(memory_space=pltpu.VMEM), pl.BlockSpec(memory_space=pl.ANY)
+    dma = pltpu.SemaphoreType.DMA
+    return pl.pallas_call(
+        functools.partial(kernel, plan, n_tp, here, experts),
+        out_shape=jax.ShapeDtypeStruct((rows, width), BF16),
+        in_specs=[hbm, vmem, vmem, hbm, hbm] + [hbm] * 6,
+        out_specs=vmem,
+        scratch_shapes=[
+            pltpu.VMEM((n_ep, n_tp, rows, width), BF16),
+            pltpu.VMEM((here, n_ep * cap, full), BF16),
+            pltpu.VMEM((n_ep, here * cap, rows), BF16),
+            pltpu.VMEM((here, n_ep * cap, 1), F32),
+            pltpu.VMEM((slots, rows), F32),
+            pltpu.VMEM((n_tp, rows, width), F32),
+            pltpu.VMEM((n_tp, slots, width), BF16),
+            pltpu.VMEM((n_ep,) + ids.shape, jnp.int32),
+            pltpu.VMEM((2, full, hid), BF16),
+            pltpu.VMEM((2, full, hid), BF16),
+            pltpu.VMEM((2, hid, full), BF16),
+            pltpu.VMEM((full, shid), BF16),
+            pltpu.VMEM((full, shid), BF16),
+            pltpu.VMEM((shid, full), BF16),
+            pltpu.VMEM((plan.slot_rows, width), BF16),
+            pltpu.VMEM((n_ep, n_tp // 2, rows, width), BF16),
+            dma((3,)), dma((3, 2)), dma((3,)),
+            dma((len(plan.sends),)), dma((len(plan.recvs),)), dma((len(plan.pair),)), dma((len(plan.pair),)),
+            dma((len(plan.back),)), dma((len(plan.slots),)), dma((len(plan.back),)), dma((len(plan.back),)),
+        ],
+        compiler_params=pltpu.CompilerParams(
+            collective_id=0, has_side_effects=True, vmem_limit_bytes=67043328),
+    )(tokens, norm_gain.reshape(1, full), shared_gate_w.reshape(1, full), rt, ids, w_gate, w_up, w_down,
+      shared_w_gate, shared_w_up, shared_w_down)
+
+
+def fits(mesh, tokens, norm_gain, router_weight, shared_gate_w, expert_ids, w_gate, *rest):
+    rows, width = tokens.shape
+    n_ep, n_tp = mesh.shape["ep"], mesh.shape["tp"]
+    return (
+        n_ep in (4, 8)
+        and n_tp == 4
+        and rows % 256 == 0
+        and width % 128 == 0
+        and w_gate.shape[0] % 8 == 0
+        and rows * width <= 1 << 17
+        and w_gate.shape[0] * w_gate.shape[1] * w_gate.shape[2] <= 6 << 20
+        and rest[2].shape[0] * rest[2].shape[1] <= 3 << 19
+    )
 
 
 def send_back(summed):
@@ -162,6 +576,8 @@
 def solution(mesh):
     def per_device(tokens, *rest):
         gathered = mesh.size * tokens.size * tokens.dtype.itemsize
+        if gathered <= 16 << 20 and fits(mesh, tokens, *rest):
+            return fused_plan(mesh, tokens, *rest)
         plan = gather_plan if gathered <= 16 << 20 else dispatch_plan
         return plan(tokens, *rest)
 

time: 322 us -> 176 us (0.55)
  Pallas kernels: 0 us -> 128 us
  waiting for transfers between devices: 111 us -> 0 us
  blocking collectives: 93.7 us -> 0 us
  matrix products: 64.8 us -> 0 us
  local copies, waits for them, and re-layouts: 22.7 us -> 46.5 us
  other arithmetic: 15.5 us -> 0 us
  between operations: 13.5 us -> 0.01 us
    pallas_call x0 -> x1, Pallas kernels: none -> 128 us  [fused_plan(): pl.pallas_call(functools.partial(kernel, plan, n_tp, here, experts), out_...]
    reduce_scatter x1 -> x0, waiting for transfers between devices: 70.2 us -> none  [gather_plan(): total = lax.psum_scatter(total, 'tp', scatter_dimension=2, tiled=True)]
    dot_general x8 -> x0, matrix products: 58.7 us -> none  [the longest x1 14.6 us: gather_plan(): up = jnp.einsum('jskd,jdf->jskf', x, w_up, preferred_element_type=F32)]
    all_to_all x1 -> x0, blocking collectives: 53.7 us -> none  [gather_plan(): terms = lax.all_to_all(total, 'ep', split_axis=0, concat_axis=0, tiled=True)]
    all_gather x1 -> x0, waiting for transfers between devices: 40.2 us -> none  [gather_plan(): every = lax.all_gather(tokens, ('ep', 'tp'), axis=0)]
    all_gather x2 -> x0, blocking collectives: 40 us -> none  [the longest x1 32.6 us: gather_plan(): ids = lax.all_gather(expert_ids.reshape(-1), 'ep', axis=0)]
    unnamed x13 -> x5, local copies, waits for them, and re-layouts: 2.88 us -> 42.5 us
    convert_element_type x1 -> x0, local copies, waits for them, and re-layouts: 11.5 us -> none  [gather_plan(): values = whole.reshape(n_ep, rows, full).astype(F32)]
  transfers between devices with their start and end apart: 2 -> 0, of which waited for: 2 -> 0; matrix products, arithmetic and copies ran while one was open for 1% -> 0% of each run, Pallas kernels for 0% -> 0%
where the time goes in v1:
time: 176 us; the launch traced here: 175 us
  Pallas kernels  128 us (73%)
  local copies, waits for them, and re-layouts  46.5 us (26%)
    pallas_call x1, Pallas kernels, fused_plan(): pl.pallas_call(functools.partial(kernel, plan, n_tp, here, experts), out_...  128 us
    unnamed x5, local copies, waits for them, and re-layouts  42.5 us

profile of v1, /device:TPU:0, one launch (start us, length us, event | category | flops | bytes accessed | tf_op | source)
XLA Modules:
  0.0 174.9 jit_solution(18134703006345156909)
XLA Ops:
  0.0 1.3 reshape.7.sgw
  1.3 1.3 pad.9.ids
  2.6 1.5 pad.8.rt
  4.0 4.6 %copy.14.swg = bf16[2048,704]{1,0:T(8,128)(2,1)} copy(bf16[2048,704]{0,1:T(8,128)(2,1)} %param.19) | data formatting | bytes 5767168 | tf_op args[8]
  8.7 4.6 %copy.15.swu = bf16[2048,704]{1,0:T(8,128)(2,1)} copy(bf16[2048,704]{0,1:T(8,128)(2,1)} %param.20) | data formatting | bytes 5767168 | tf_op args[9]
  13.3 16.2 %copy.12.wg = bf16[8,2048,352]{2,1,0:T(8,128)(2,1)} copy(bf16[8,2048,352]{1,2,0:T(8,128)(2,1)} %param.16) | data formatting | bytes 23068672 | tf_op args[5]
  29.5 15.3 %copy.13.wu = bf16[8,2048,352]{2,1,0:T(8,128)(2,1)} copy(bf16[8,2048,352]{1,2,0:T(8,128)(2,1)} %param.17) | data formatting | bytes 23068672 | tf_op args[6]
  44.9 128.3 %shard_map.109 = bf16[256,512]{1,0:T(8,128)(2,1)} custom-call(bf16[256,512]{1,0:T(8,128)(2,1)} %tok.1, f32[1,2048]{1,0:T(1,128)} %bitcast.4, bf16[1,2048]{1,0:T(2,128)(2,1)} %reshape.7.sgw, bf16[64,512]{1,0:T(8,128)(2,1)} %pad.8.rt, s32[8,256]{1,0:T(8,128)} %pad.9.ids, bf16[8,2048,352]{2,1,0:T(8,128)(2,1)} %copy.12.wg, bf16[8,2048,352]{2,1,0:T(8,128)(2,1)} %copy.13.wu, ...), custom_call_target="tpu_custom_call" | custom-call | tf_op jit(solution)/shard_map/pallas_call | solution.py:377
  173.2 1.7 copy.17

commit v2 on v1

--- a/solution.py
+++ b/solution.py
@@ -97,7 +97,7 @@
 
 def kernel(plan, n_tp, here, experts,
            tok, gain, sgw, rt, ids, wg, wu, wd, swg, swu, swd, out,
-           g, xs, pick, sw, pr, part, rbuf, idb, wgb, wub, wdb, sgb, sub, sdb, slot, cbuf,
+           g, xs, pick, sw, pr, part, rbuf, idb, wab, wdb, sab, sdb, mine, slot, cbuf,
            loc, wsem, ssem, send, recv, psend, precv, bsend, brecv, bpsend, bprecv):
     nz = plan.nz
     ep, tp = lax.axis_index("ep"), lax.axis_index("tp")
@@ -139,14 +139,18 @@
     ]
     for cp in own:
         cp.start()
+    hid, shid = wg.shape[1], swg.shape[0]
     shared_copies = [
-        pltpu.make_async_copy(a, b, ssem.at[i]) for i, (a, b) in enumerate(((swg, sgb), (swu, sub), (swd, sdb)))
+        pltpu.make_async_copy(swg, sab.at[0:shid], ssem.at[0]),
+        pltpu.make_async_copy(swu, sab.at[shid:2 * shid], ssem.at[1]),
+        pltpu.make_async_copy(swd, sdb, ssem.at[2]),
     ]
 
     def weights(j, buf):
         return [
-            pltpu.make_async_copy(a.at[j], b.at[buf], wsem.at[i, buf])
-            for i, (a, b) in enumerate(((wg, wgb), (wu, wub), (wd, wdb)))
+            pltpu.make_async_copy(wg.at[j], wab.at[buf, 0:hid], wsem.at[0, buf]),
+            pltpu.make_async_copy(wu.at[j], wab.at[buf, hid:2 * hid], wsem.at[1, buf]),
+            pltpu.make_async_copy(wd.at[j], wdb.at[buf], wsem.at[2, buf]),
         ]
 
     for cp in shared_copies + weights(0, 0) + weights(1, 1):
@@ -216,7 +220,7 @@
     for k, off in plan.events:
         when(valid(off), lambda k=k, off=off: finish(k, off))
 
-    slots = n_ep * here
+    pr[...] = jnp.zeros_like(pr)
 
     @pl.loop(0, n_ep)
     def _(s):
@@ -225,22 +229,19 @@
             v = g[s, t].astype(F32)
             total = total + jnp.sum(v * v, axis=-1, keepdims=True)
         inv = lax.rsqrt(total / (n_tp * width) + 1e-6)
-        logits = jnp.zeros((slots, rows), F32)
+        logits = jnp.zeros((experts, rows), F32)
         for t in range(n_tp):
             v = g[s, t].astype(F32) * inv * gain[:, t * width:(t + 1) * width]
             v = v.astype(BF16)
             g[s, t] = v
             logits = logits + lax.dot_general(rbuf[t], v, (((1,), (1,)), ((), ())), preferred_element_type=F32)
-        names = lax.broadcasted_iota(jnp.int32, (slots, rows), 0)
-        logits = jnp.where(names < experts, logits, -1e30)
         ex = jnp.exp(logits - jnp.max(logits, axis=0, keepdims=True))
-        ex = jnp.where(names < experts, ex, 0.0)
-        pr[...] = ex / jnp.sum(ex, axis=0, keepdims=True)
+        pr[0:experts, :] = ex / jnp.sum(ex, axis=0, keepdims=True)
         probs = pr[pl.ds(pl.multiple_of(ep * here, here), here), :]
-        mine = ep * here + lax.broadcasted_iota(jnp.int32, (here, rows), 0)
+        names = ep * here + lax.broadcasted_iota(jnp.int32, (here, rows), 0)
         match = jnp.zeros((here, rows), jnp.bool_)
         for q in range(ids.shape[0]):
-            match = jnp.logical_or(match, mine == idb[s, q:q + 1, :])
+            match = jnp.logical_or(match, names == idb[s, q:q + 1, :])
         hit = jnp.where(match, 1.0, 0.0)
         upper = jnp.where(
             lax.broadcasted_iota(jnp.int32, (rows, rows), 0) < lax.broadcasted_iota(jnp.int32, (rows, rows), 1), 1.0, 0.0)
@@ -259,30 +260,30 @@
 
     for cp in shared_copies:
         cp.wait()
-    sg = jnp.zeros((rows, sgb.shape[1]), F32)
-    su = jnp.zeros((rows, sgb.shape[1]), F32)
     gate = jnp.zeros((rows, 1), F32)
     for t in range(n_tp):
         v = g[ep, t]
-        sg = sg + jnp.dot(v, sgb[t * width:(t + 1) * width, :], preferred_element_type=F32)
-        su = su + jnp.dot(v, sub[t * width:(t + 1) * width, :], preferred_element_type=F32)
+        mine[:, t * width:(t + 1) * width] = v
         gate = gate + jnp.sum(v.astype(F32) * sgw[:, t * width:(t + 1) * width].astype(F32), axis=-1, keepdims=True)
-    sh = (sg / (1.0 + jnp.exp(-sg)) * su).astype(BF16)
+    ab = lax.dot_general(sab[...], mine[...], (((1,), (1,)), ((), ())), preferred_element_type=F32)
+    a, b = ab[:shid], ab[shid:]
+    h = (a / (1.0 + jnp.exp(-a)) * b).astype(BF16)
     gate = 1.0 / (1.0 + jnp.exp(-gate))
     for t in range(n_tp):
-        part[t] = gate * jnp.dot(sh, sdb[:, t * width:(t + 1) * width], preferred_element_type=F32)
+        part[t] = gate * lax.dot_general(
+            h, sdb[:, t * width:(t + 1) * width], (((0,), (0,)), ((), ())), preferred_element_type=F32)
 
     @pl.loop(0, here)
     def _(j):
         buf = j % 2
         for cp in weights(j, buf):
             cp.wait()
-        v = xs[j]
-        a = jnp.dot(v, wgb[buf], preferred_element_type=F32)
-        b = jnp.dot(v, wub[buf], preferred_element_type=F32)
+        ab = lax.dot_general(wab[buf], xs[j], (((1,), (1,)), ((), ())), preferred_element_type=F32)
+        a, b = ab[:hid], ab[hid:]
         h = (a / (1.0 + jnp.exp(-a)) * b).astype(BF16)
         for t in range(n_tp):
-            o = jnp.dot(h, wdb[buf, :, t * width:(t + 1) * width], preferred_element_type=F32)
+            o = lax.dot_general(
+                h, wdb[buf, :, t * width:(t + 1) * width], (((0,), (0,)), ((), ())), preferred_element_type=F32)
             xs[j, :, t * width:(t + 1) * width] = (o * sw[j]).astype(BF16)
 
         @pl.when(j + 2 < here)
@@ -337,8 +338,8 @@
             _, start, n = plan.every[k]
             zs, xx, yy = z - off[0], (x + off[1]) % 2, (y + off[2]) % 2
             pair_back(k, off, c).wait_recv()
-            mine = place(k, off, c)
-            acc = mine[...].astype(F32) + cbuf[zs * 2 + xx, yy, start:start + n, :].astype(F32)
+            held = place(k, off, c)
+            acc = held[...].astype(F32) + cbuf[zs * 2 + xx, yy, start:start + n, :].astype(F32)
             for hop in next_hops(plan.every[k][0], off, nz):
                 cp, ref = child_copy(k, off, hop)
                 if hop in exists:
@@ -350,7 +351,7 @@
             if off == (0, 0, 0):
                 out[start:start + n, :] = acc.astype(BF16)
             else:
-                mine[...] = acc.astype(BF16)
+                held[...] = acc.astype(BF16)
                 parent(k, off).start()
         when(valid(off), step)
     for k, off in plan.back:
@@ -370,8 +371,8 @@
     shid = shared_w_gate.shape[1]
     slots, cap = n_ep * here, rows // 8
     plan = Plan(n_ep, rows)
-    rt = jnp.pad(router_weight.T, ((0, slots - experts), (0, 0)))
-    ids = jnp.pad(expert_ids.T, ((0, -expert_ids.shape[1] % 8), (0, 0)), constant_values=-1)
+    rt = router_weight.T
+    ids = expert_ids.T
     vmem, hbm = pl.BlockSpec(memory_space=pltpu.VMEM), pl.BlockSpec(memory_space=pl.ANY)
     dma = pltpu.SemaphoreType.DMA
     return pl.pallas_call(
@@ -386,14 +387,13 @@
             pltpu.VMEM((here, n_ep * cap, 1), F32),
             pltpu.VMEM((slots, rows), F32),
             pltpu.VMEM((n_tp, rows, width), F32),
-            pltpu.VMEM((n_tp, slots, width), BF16),
+            pltpu.VMEM((n_tp, experts, width), BF16),
             pltpu.VMEM((n_ep,) + ids.shape, jnp.int32),
-            pltpu.VMEM((2, full, hid), BF16),
-            pltpu.VMEM((2, full, hid), BF16),
+            pltpu.VMEM((2, 2 * hid, full), BF16),
             pltpu.VMEM((2, hid, full), BF16),
-            pltpu.VMEM((full, shid), BF16),
-            pltpu.VMEM((full, shid), BF16),
+            pltpu.VMEM((2 * shid, full), BF16),
             pltpu.VMEM((shid, full), BF16),
+            pltpu.VMEM((rows, full), BF16),
             pltpu.VMEM((plan.slot_rows, width), BF16),
             pltpu.VMEM((n_ep, n_tp // 2, rows, width), BF16),
             dma((3,)), dma((3, 2)), dma((3,)),
@@ -402,8 +402,8 @@
         ],
         compiler_params=pltpu.CompilerParams(
             collective_id=0, has_side_effects=True, vmem_limit_bytes=67043328),
-    )(tokens, norm_gain.reshape(1, full), shared_gate_w.reshape(1, full), rt, ids, w_gate, w_up, w_down,
-      shared_w_gate, shared_w_up, shared_w_down)
+    )(tokens, norm_gain.reshape(1, full), shared_gate_w.reshape(1, full), rt, ids,
+      w_gate.transpose(0, 2, 1), w_up.transpose(0, 2, 1), w_down, shared_w_gate.T, shared_w_up.T, shared_w_down)
 
 
 def fits(mesh, tokens, norm_gain, router_weight, shared_gate_w, expert_ids, w_gate, *rest):

time: 176 us -> 139 us (0.79)
  local copies, waits for them, and re-layouts: 46.5 us -> 2.96 us
  Pallas kernels: 128 us -> 136 us
    unnamed x5 -> x1, local copies, waits for them, and re-layouts: 42.5 us -> 1.67 us
    pallas_call x1, Pallas kernels: 128 us -> 136 us  [fused_plan(): pl.pallas_call(functools.partial(kernel, plan, n_tp, here, experts), out_...]
    pad x2 -> x0, local copies, waits for them, and re-layouts: 2.76 us -> none  [the longest x1 1.47 us: fused_plan(): rt = jnp.pad(router_weight.T, ((0, slots - experts), (0, 0)))]
where the time goes in v2:
time: 139 us
  Pallas kernels  136 us (98%)
  local copies, waits for them, and re-layouts  2.96 us (2%)
    pallas_call x1, Pallas kernels, fused_plan(): pl.pallas_call(functools.partial(kernel, plan, n_tp, here, experts), out_...  136 us

profile of v2, /device:TPU:0, one launch (start us, length us, event | category | flops | bytes accessed | tf_op | source)
XLA Modules:
  0.0 138.7 jit_solution(4798151140151270748)
XLA Ops:
  0.0 1.3 reshape.7.sgw
  1.3 135.7 %shard_map.109 = bf16[256,512]{1,0:T(8,128)(2,1)} custom-call(bf16[256,512]{1,0:T(8,128)(2,1)} %tok.1, f32[1,2048]{1,0:T(1,128)} %bitcast.12, bf16[1,2048]{1,0:T(2,128)(2,1)} %reshape.7.sgw, bf16[60,512]{1,0:T(8,128)(2,1)} %bitcast.11, s32[4,256]{1,0:T(4,128)} %bitcast.13, bf16[8,352,2048]{2,1,0:T(8,128)(2,1)} %bitcast.7, bf16[8,352,2048]{2,1,0:T(8,128)(2,1)} %bitcast.8, ...), custom_call_target="tpu_custom_call" | custom-call | tf_op jit(solution)/shard_map/pallas_call | solution.py:378
  137.0 1.7 %copy.13 = bf16[256,512]{1,0:T(8,128)(2,1)} copy(bf16[256,512]{1,0:T(8,128)(2,1)} %shard_map.109) | data formatting | bytes 524288

commit v3 on v2

--- a/solution.py
+++ b/solution.py
@@ -97,7 +97,7 @@
 
 def kernel(plan, n_tp, here, experts,
            tok, gain, sgw, rt, ids, wg, wu, wd, swg, swu, swd, out,
-           g, xs, pick, sw, pr, part, rbuf, idb, wab, wdb, sab, sdb, mine, slot, cbuf,
+           g, xs, pick, sw, pr, part, rbuf, idb, wab, wdb, mine, nrm, hs, hb, ys, slot, cbuf,
            loc, wsem, ssem, send, recv, psend, precv, bsend, brecv, bpsend, bprecv):
     nz = plan.nz
     ep, tp = lax.axis_index("ep"), lax.axis_index("tp")
@@ -140,17 +140,25 @@
     for cp in own:
         cp.start()
     hid, shid = wg.shape[1], swg.shape[0]
+    deep = wab.shape[0] // (2 * hid)
+    top, low = 4 * hid, 2 * hid
     shared_copies = [
-        pltpu.make_async_copy(swg, sab.at[0:shid], ssem.at[0]),
-        pltpu.make_async_copy(swu, sab.at[shid:2 * shid], ssem.at[1]),
-        pltpu.make_async_copy(swd, sdb, ssem.at[2]),
+        pltpu.make_async_copy(swg, wab.at[top:top + shid], ssem.at[0]),
+        pltpu.make_async_copy(swu, wab.at[top + shid:top + 2 * shid], ssem.at[1]),
+        pltpu.make_async_copy(swd, wdb.at[low:low + shid], ssem.at[2]),
     ]
 
+    def rows_of(buf, n):
+        return pl.ds(buf * n if isinstance(buf, int) else pl.multiple_of(buf * n, 16), n)
+
     def weights(j, buf):
+        first, second = buf * (2 * hid), buf * (2 * hid) + hid
+        if not isinstance(buf, int):
+            first, second = pl.multiple_of(first, 16), pl.multiple_of(second, 16)
         return [
-            pltpu.make_async_copy(wg.at[j], wab.at[buf, 0:hid], wsem.at[0, buf]),
-            pltpu.make_async_copy(wu.at[j], wab.at[buf, hid:2 * hid], wsem.at[1, buf]),
-            pltpu.make_async_copy(wd.at[j], wdb.at[buf], wsem.at[2, buf]),
+            pltpu.make_async_copy(wg.at[j], wab.at[pl.ds(first, hid)], wsem.at[0, buf]),
+            pltpu.make_async_copy(wu.at[j], wab.at[pl.ds(second, hid)], wsem.at[1, buf]),
+            pltpu.make_async_copy(wd.at[j], wdb.at[rows_of(buf, hid)], wsem.at[2, buf]),
         ]
 
     for cp in shared_copies + weights(0, 0) + weights(1, 1):
@@ -197,10 +205,18 @@
             src_ref=ref, dst_ref=ref, send_sem=psend.at[i], recv_sem=precv.at[i],
             device_id=to["c"], device_id_type=MESH)
 
-    for k, off in plan.events:
+    near = [sorted(range(nz), key=lambda v, p=p: abs(v - p)) for p in range(nz)]
+
+    def ranked(rank):
+        value = near[nz - 1][rank]
+        for p in range(nz - 1):
+            value = jnp.where(z == p, near[p][rank], value)
+        return value
+
+    def forward(k, off):
         order = plan.every[k][0]
 
-        def step(k=k, off=off, order=order):
+        def step():
             if off != (0, 0, 0):
                 arrival(k, off).wait_recv()
             for hop in next_hops(order, off, nz):
@@ -210,20 +226,14 @@
 
         when(valid(off), step)
 
-    def finish(k, off):
-        for hop in next_hops(plan.every[k][0], off, nz):
-            when([exists[hop]] if hop in exists else [], lambda: hop_copy(k, off, hop).wait_send())
-        if k != 0:
-            pair_copy(k, off, 1 - c).wait_recv()
-            pair_copy(k, off, c).wait_send()
-
-    for k, off in plan.events:
-        when(valid(off), lambda k=k, off=off: finish(k, off))
-
     pr[...] = jnp.zeros_like(pr)
 
-    @pl.loop(0, n_ep)
-    def _(s):
+    def source(rank, dx):
+        for k, off in plan.events:
+            if (k >= 2 and abs(off[0]) == rank and off[1] == dx) or (k == 1 and rank == 0 and dx == 0):
+                when(valid(off), lambda k=k, off=off: pair_copy(k, off, 1 - c).wait_recv())
+        s = ranked(rank) * 2 + (x + dx) % 2
+        normed = mine if (rank, dx) == (0, 0) else nrm
         total = jnp.zeros((rows, 1), F32)
         for t in range(n_tp):
             v = g[s, t].astype(F32)
@@ -231,9 +241,9 @@
         inv = lax.rsqrt(total / (n_tp * width) + 1e-6)
         logits = jnp.zeros((experts, rows), F32)
         for t in range(n_tp):
-            v = g[s, t].astype(F32) * inv * gain[:, t * width:(t + 1) * width]
-            v = v.astype(BF16)
-            g[s, t] = v
+            cols = slice(t * width, (t + 1) * width)
+            v = (g[s, t].astype(F32) * inv * gain[:, cols]).astype(BF16)
+            normed[:, cols] = v
             logits = logits + lax.dot_general(rbuf[t], v, (((1,), (1,)), ((), ())), preferred_element_type=F32)
         ex = jnp.exp(logits - jnp.max(logits, axis=0, keepdims=True))
         pr[0:experts, :] = ex / jnp.sum(ex, axis=0, keepdims=True)
@@ -245,60 +255,106 @@
         hit = jnp.where(match, 1.0, 0.0)
         upper = jnp.where(
             lax.broadcasted_iota(jnp.int32, (rows, rows), 0) < lax.broadcasted_iota(jnp.int32, (rows, rows), 1), 1.0, 0.0)
-        rank = jnp.dot(hit.astype(BF16), upper.astype(BF16), preferred_element_type=F32)
-        spot = jnp.where(match, rank, -1.0).astype(jnp.int32)
+        order_rank = jnp.dot(hit.astype(BF16), upper.astype(BF16), preferred_element_type=F32)
+        spot = jnp.where(match, order_rank, -1.0).astype(jnp.int32)
         spots = lax.broadcasted_iota(jnp.int32, (cap, rows), 0)
+        span = pl.ds(pl.multiple_of(s * cap, cap), cap)
         for j in range(here):
             one = spot[j:j + 1, :] == spots
-            sw[j, pl.ds(pl.multiple_of(s * cap, cap), cap), :] = jnp.sum(
-                jnp.where(one, probs[j:j + 1, :], 0.0), axis=1, keepdims=True)
+            sw[j, span, :] = jnp.sum(jnp.where(one, probs[j:j + 1, :], 0.0), axis=1, keepdims=True)
             pick[s, j * cap:(j + 1) * cap, :] = jnp.where(one, 1.0, 0.0).astype(BF16)
         for t in range(n_tp):
-            v = jnp.dot(pick[s], g[s, t], preferred_element_type=F32).astype(BF16)
+            cols = slice(t * width, (t + 1) * width)
+            v = jnp.dot(pick[s], normed[:, cols], preferred_element_type=F32).astype(BF16)
             for j in range(here):
-                xs[j, pl.ds(pl.multiple_of(s * cap, cap), cap), t * width:(t + 1) * width] = v[j * cap:(j + 1) * cap]
-
-    for cp in shared_copies:
+                xs[j, span, cols] = v[j * cap:(j + 1) * cap]
+
+    def shared_hidden():
+        for cp in shared_copies:
+            cp.wait()
+        ab = lax.dot_general(
+            wab[top:top + 2 * shid], mine[...], (((1,), (1,)), ((), ())), preferred_element_type=F32)
+        a, b = ab[:shid], ab[shid:]
+        hs[...] = (a / (1.0 + jnp.exp(-a)) * b).astype(BF16)
+
+    def shared_out():
+        gate = jnp.zeros((rows, 1), F32)
+        for t in range(n_tp):
+            cols = slice(t * width, (t + 1) * width)
+            gate = gate + jnp.sum(
+                mine[:, cols].astype(F32) * sgw[:, cols].astype(F32), axis=-1, keepdims=True)
+        gate = 1.0 / (1.0 + jnp.exp(-gate))
+        for t in range(n_tp):
+            cols = slice(t * width, (t + 1) * width)
+            part[t] = gate * lax.dot_general(
+                hs[...], wdb[low:low + shid, cols], (((0,), (0,)), ((), ())), preferred_element_type=F32)
+        for j in range(2, min(deep, here)):
+            for cp in weights(j, j):
+                cp.start()
+
+    last = {}
+    for i, (k, off) in enumerate(plan.events):
+        rank, dx = abs(off[0]), off[1]
+        for r in range(rank, nz):
+            if k >= 2:
+                last[r, dx] = i
+            else:
+                for both in (0, 1):
+                    last[r, both] = i
+    points = sorted(last, key=lambda r: (last[r], r))
+    pieces = []
+    for r in points:
+        pieces.append((last[r] + 1000, functools.partial(source, *r)))
+        if r == (0, 0):
+            pieces.append((last[r] + 8, shared_hidden))
+            pieces.append((last[r] + 12, shared_out))
+    for i, (k, off) in enumerate(plan.events):
+        forward(k, off)
+        if pieces and pieces[0][0] <= i:
+            pieces.pop(0)[1]()
+    for _, piece in pieces:
+        piece()
+
+    def finish(k, off):
+        for hop in next_hops(plan.every[k][0], off, nz):
+            when([exists[hop]] if hop in exists else [], lambda: hop_copy(k, off, hop).wait_send())
+        if k != 0:
+            pair_copy(k, off, c).wait_send()
+
+    for k, off in plan.events:
+        when(valid(off), lambda k=k, off=off: finish(k, off))
+
+    def hidden(j):
+        ab = lax.dot_general(
+            wab[rows_of(j % deep, 2 * hid)], xs[j], (((1,), (1,)), ((), ())), preferred_element_type=F32)
+        a, b = ab[:hid], ab[hid:]
+        return (a / (1.0 + jnp.exp(-a)) * b).astype(BF16)
+
+    def down(j, h):
+        for t in range(n_tp):
+            cols = slice(t * width, (t + 1) * width)
+            o = lax.dot_general(
+                h, wdb[rows_of(j % deep, hid), cols], (((0,), (0,)), ((), ())), preferred_element_type=F32)
+            ys[j, :, cols] = (o * sw[j]).astype(BF16)
+
+    for cp in weights(0, 0):
         cp.wait()
-    gate = jnp.zeros((rows, 1), F32)
-    for t in range(n_tp):
-        v = g[ep, t]
-        mine[:, t * width:(t + 1) * width] = v
-        gate = gate + jnp.sum(v.astype(F32) * sgw[:, t * width:(t + 1) * width].astype(F32), axis=-1, keepdims=True)
-    ab = lax.dot_general(sab[...], mine[...], (((1,), (1,)), ((), ())), preferred_element_type=F32)
-    a, b = ab[:shid], ab[shid:]
-    h = (a / (1.0 + jnp.exp(-a)) * b).astype(BF16)
-    gate = 1.0 / (1.0 + jnp.exp(-gate))
-    for t in range(n_tp):
-        part[t] = gate * lax.dot_general(
-            h, sdb[:, t * width:(t + 1) * width], (((0,), (0,)), ((), ())), preferred_element_type=F32)
-
-    @pl.loop(0, here)
+    hb[...] = hidden(0)
+
+    @pl.loop(1, here)
     def _(j):
-        buf = j % 2
-        for cp in weights(j, buf):
+        for cp in weights(j, j % deep):
             cp.wait()
-        ab = lax.dot_general(wab[buf], xs[j], (((1,), (1,)), ((), ())), preferred_element_type=F32)
-        a, b = ab[:hid], ab[hid:]
-        h = (a / (1.0 + jnp.exp(-a)) * b).astype(BF16)
-        for t in range(n_tp):
-            o = lax.dot_general(
-                h, wdb[buf, :, t * width:(t + 1) * width], (((0,), (0,)), ((), ())), preferred_element_type=F32)
-            xs[j, :, t * width:(t + 1) * width] = (o * sw[j]).astype(BF16)
-
-        @pl.when(j + 2 < here)
+        before = hb[...]
+        hb[...] = hidden(j)
+        down(j - 1, before)
+
+        @pl.when(j - 1 + deep < here)
         def _():
-            for cp in weights(j + 2, buf):
+            for cp in weights(j - 1 + deep, (j - 1) % deep):
                 cp.start()
 
-    @pl.loop(0, n_ep)
-    def _(s):
-        for t in range(n_tp):
-            v = xs[:, pl.ds(pl.multiple_of(s * cap, cap), cap), t * width:(t + 1) * width]
-            v = v.reshape(here * cap, width)
-            o = lax.dot_general(pick[s], v, (((0,), (0,)), ((), ())), preferred_element_type=F32)
-            o = o + jnp.where(s == ep, part[t], 0.0)
-            g[s, t] = o.astype(BF16)
+    down(here - 1, hb[...])
 
     def pair_back(k, off, core):
         ref = place(k, off, core)
@@ -331,9 +387,26 @@
             send_sem=bsend.at[plan.parents[k, off]], recv_sem=brecv.at[i],
             device_id=to[hop], device_id_type=MESH)
 
-    for k, off in plan.back:
-        when(valid(off), lambda k=k, off=off: pair_back(k, off, 1 - c).start())
-    for k, off in plan.back:
+    def tokens_of(rank, dx):
+        s = ranked(nz - 1 - rank) * 2 + (x + dx) % 2
+        span = pl.ds(pl.multiple_of(s * cap, cap), cap)
+        for t in range(n_tp):
+            v = ys[:, span, t * width:(t + 1) * width].reshape(here * cap, width)
+            o = lax.dot_general(pick[s], v, (((0,), (0,)), ((), ())), preferred_element_type=F32)
+            if rank == nz - 1 and dx == 0:
+                o = o + part[t]
+            g[s, t] = o.astype(BF16)
+        for k, off in plan.back:
+            if abs(off[0]) == nz - 1 - rank and off[1] == dx:
+                when(valid(off), lambda k=k, off=off: pair_back(k, off, 1 - c).start())
+
+    todo = [(rank, dx) for rank in range(nz) for dx in (1, 0)]
+    for i, (k, off) in enumerate(plan.back):
+        while todo and (i % 3 == 0 or (nz - 1 - abs(off[0]), off[1]) in todo):
+            tokens_of(*todo.pop(0))
+            if (nz - 1 - abs(off[0]), off[1]) not in todo:
+                break
+
         def step(k=k, off=off):
             _, start, n = plan.every[k]
             zs, xx, yy = z - off[0], (x + off[1]) % 2, (y + off[2]) % 2
@@ -389,14 +462,16 @@
             pltpu.VMEM((n_tp, rows, width), F32),
             pltpu.VMEM((n_tp, experts, width), BF16),
             pltpu.VMEM((n_ep,) + ids.shape, jnp.int32),
-            pltpu.VMEM((2, 2 * hid, full), BF16),
-            pltpu.VMEM((2, hid, full), BF16),
-            pltpu.VMEM((2 * shid, full), BF16),
-            pltpu.VMEM((shid, full), BF16),
+            pltpu.VMEM((8 * hid, full), BF16),
+            pltpu.VMEM((4 * hid, full), BF16),
             pltpu.VMEM((rows, full), BF16),
+            pltpu.VMEM((rows, full), BF16),
+            pltpu.VMEM((shid, rows), BF16),
+            pltpu.VMEM((hid, n_ep * cap), BF16),
+            pltpu.VMEM((here, n_ep * cap, full), BF16),
             pltpu.VMEM((plan.slot_rows, width), BF16),
             pltpu.VMEM((n_ep, n_tp // 2, rows, width), BF16),
-            dma((3,)), dma((3, 2)), dma((3,)),
+            dma((3,)), dma((3, 4)), dma((3,)),
             dma((len(plan.sends),)), dma((len(plan.recvs),)), dma((len(plan.pair),)), dma((len(plan.pair),)),
             dma((len(plan.back),)), dma((len(plan.slots),)), dma((len(plan.back),)), dma((len(plan.back),)),
         ],
@@ -417,7 +492,9 @@
         and w_gate.shape[0] % 8 == 0
         and rows * width <= 1 << 17
         and w_gate.shape[0] * w_gate.shape[1] * w_gate.shape[2] <= 6 << 20
-        and rest[2].shape[0] * rest[2].shape[1] <= 3 << 19
+        and rest[2].shape[1] <= 2 * w_gate.shape[2]
+        and w_gate.shape[2] % 16 == 0
+        and w_gate.shape[0] >= 4
     )
 
 

time: 139 us -> 126 us (0.906)
  Pallas kernels: 136 us -> 123 us
    pallas_call x1, Pallas kernels: 136 us -> 123 us  [fused_plan(): pl.pallas_call(functools.partial(kernel, plan, n_tp, here, experts), out_...]
where the time goes in v3:
time: 126 us
  Pallas kernels  123 us (98%)
  local copies, waits for them, and re-layouts  2.96 us (2%)
    pallas_call x1, Pallas kernels, fused_plan(): pl.pallas_call(functools.partial(kernel, plan, n_tp, here, experts), out_...  123 us

profile of v3, /device:TPU:0, one launch (start us, length us, event | category | flops | bytes accessed | tf_op | source)
XLA Modules:
  0.0 125.6 jit_solution(4493451103541412567)
XLA Ops:
  0.0 1.3 %reshape.7.sgw = bf16[1,2048]{1,0:T(2,128)(2,1)} reshape(bf16[2048]{0:T(1024)(128)(2,1)} %param.14) | data formatting | bytes 8192 | tf_op jit(solution)/shard_map/reshape | solution.py:480
  1.3 122.7 %shard_map.109 = bf16[256,512]{1,0:T(8,128)(2,1)} custom-call(bf16[256,512]{1,0:T(8,128)(2,1)} %tok.1, f32[1,2048]{1,0:T(1,128)} %bitcast.12, bf16[1,2048]{1,0:T(2,128)(2,1)} %reshape.7.sgw, bf16[60,512]{1,0:T(8,128)(2,1)} %bitcast.11, s32[4,256]{1,0:T(4,128)} %bitcast.13, bf16[8,352,2048]{2,1,0:T(8,128)(2,1)} %bitcast.7, bf16[8,352,2048]{2,1,0:T(8,128)(2,1)} %bitcast.8, ...), custom_call_target="tpu_custom_call" | custom-call | tf_op jit(solution)/shard_map/pallas_call | solution.py:451
  124.0 1.7 %copy.13 = bf16[256,512]{1,0:T(8,128)(2,1)} copy(bf16[256,512]{1,0:T(8,128)(2,1)} %shard_map.109) | data formatting | bytes 524288
